TPU v7x, 256 devices: a 4x2x16 block of a 4x16x16 slice. The times are simulated.
256 devices in a mesh: groups: 2 (over y), freq: 128 (over z, x, core).
Axes of the slice: x: 4, y: 2, z: 16, core: 2. Of those that a mesh axis runs over, the one named last changes fastest.
The devices are a block of a 4x16x16 slice.
Arguments:
- primary_one: bfloat16 [1024, 512, 512], P(('groups', 'freq')), parts along dimension 0, may hold values from -6 to 6
- primary_two: bfloat16 [1024, 512, 512], P(('groups', 'freq')), parts along dimension 0, may hold values from -6 to 6
- primary_three: bfloat16 [1024, 512, 512], P(('groups', 'freq')), parts along dimension 0, may hold values from -6 to 6
- window_start: int32 [3, 1024, 512], P(None, ('groups', 'freq')), parts along dimension 1, may hold values from 0 to 255
- window_end: int32 [3, 1024, 512], P(None, ('groups', 'freq')), parts along dimension 1, may hold values from 257 to 512
Outputs:
- predicted: bfloat16 [1024, 512, 512], P(('groups', 'freq')), parts along dimension 0
There are 2 independent parts, one for each index of `groups`. A program takes and returns all parts, laid end to end along the dimension named above; each array names one. Nothing has to cross between parts.
Inputs may be any that keep to these rules, and one draw needn't show every extreme that they name: window_start of a trace is below its window_end.
All inputs are finite; a program needn't handle non-finite values.
Results may differ from a plain program's by a relative error of at most 0.0089.
Values may be sent and summed in bfloat16 or wider, within the bound.
No kernel may reach another device: no remote copies, remote signals or barrier semaphores. Data moves between devices by JAX's collectives and lax.ppermute only.
A program may use at most 64 MiB of HBM per device.

v0:
```python
import jax
import jax.numpy as jnp
from jax import lax
from jax.sharding import PartitionSpec as P

F_DEV = 1


def sent_together(arrays, axis, split_dim, concat_dim, along):
    widths = [a.shape[along] for a in arrays]
    both = jnp.concatenate(arrays, axis=along)
    whole = lax.all_to_all(both, axis, split_axis=split_dim, concat_axis=concat_dim, tiled=True)
    return tuple(jnp.split(whole, [sum(widths[:k]) for k in range(1, len(widths))], axis=along))


def make_table(count, samples):
    waves = jnp.arange(1, count + 1, dtype=jnp.int32)[:, None]
    times = jnp.arange(samples, dtype=jnp.int32)[None, :]
    phase = waves * times % samples
    angle = 2.0 * jnp.pi / samples * phase.astype(jnp.float32)
    both = jnp.stack([jnp.cos(angle), -jnp.sin(angle)], axis=1)
    return both.reshape(2 * count, samples).astype(jnp.bfloat16)


def spectrum(traces, start, finish, table, count):
    sources, receivers, samples = traces.shape
    times = jnp.arange(samples, dtype=jnp.int32)
    inside = (times >= start[:, :, None]) & (times < finish[:, :, None])
    windowed = jnp.where(inside, traces, jnp.zeros_like(traces))
    flat = windowed.reshape(sources * receivers, samples)
    spec = lax.dot_general(
        table, flat, (((1,), (1,)), ((), ())), preferred_element_type=jnp.float32
    )
    spec = spec * (1.0 / jnp.sqrt(jnp.float32(samples)))
    return spec.astype(jnp.bfloat16).reshape(count, 2, sources, receivers)


def correlate(first, second):
    swapped = jnp.stack([first[:, 1], -first[:, 0]], axis=1)
    left = jnp.stack([first, swapped], axis=1)
    cross = jnp.einsum("fkcsr,fcur->fksu", left, second, preferred_element_type=jnp.float32)
    cross = cross * (1.0 / jnp.sqrt(jnp.float32(first.shape[3])))
    return cross.astype(jnp.bfloat16)


def convolve(cross, third):
    right = jnp.stack(
        [
            jnp.stack([third[:, 0], -third[:, 1]], axis=1),
            jnp.stack([third[:, 1], third[:, 0]], axis=1),
        ],
        axis=1,
    )
    multiple = jnp.einsum("fcsu,fkcur->fksr", cross, right, preferred_element_type=jnp.float32)
    multiple = multiple * (1.0 / jnp.sqrt(jnp.float32(third.shape[2])))
    return multiple.astype(jnp.bfloat16)


def on_device(primary_one, primary_two, primary_three, window_start, window_end):
    samples = primary_one.shape[2]
    count = F_DEV * lax.axis_size("freq")
    table = make_table(count, samples)
    spec_one = spectrum(primary_one, window_start[0], window_end[0], table, count)
    spec_two = spectrum(primary_two, window_start[1], window_end[1], table, count)
    spec_three = spectrum(primary_three, window_start[2], window_end[2], table, count)
    first, second = sent_together((spec_one, spec_two), "freq", 0, 2, 1)
    cross = correlate(first, second)
    third = lax.all_to_all(spec_three, "freq", split_axis=0, concat_axis=2, tiled=True)
    multiple = convolve(cross, third)
    piece = lax.all_to_all(multiple, "freq", split_axis=2, concat_axis=0, tiled=True)
    waves, parts, sources, receivers = piece.shape
    flat = piece.reshape(waves * parts, sources * receivers)
    timed = lax.dot_general(
        flat, table, (((0,), (0,)), ((), ())), preferred_element_type=jnp.float32
    )
    timed = timed * (1.0 / jnp.sqrt(jnp.float32(count)))
    return timed.astype(jnp.bfloat16).reshape(sources, receivers, samples)


def solution(mesh):
    return jax.shard_map(
        on_device,
        mesh=mesh,
        in_specs=(
            P(("groups", "freq"), None, None),
            P(("groups", "freq"), None, None),
            P(("groups", "freq"), None, None),
            P(None, ("groups", "freq"), None),
            P(None, ("groups", "freq"), None),
        ),
        out_specs=P(("groups", "freq"), None, None),
        check_vma=False,
    )
```

profile of v0, /device:TPU:35, one launch (start us, length us, event | category | flops | bytes accessed | tf_op | source)
XLA Modules:
  0.0 282.8 jit_solution(12625566358384556773)
XLA Ops:
  0.0 0.7 slice_bitcast_fusion.3
  0.7 0.7 slice_bitcast_fusion.2
  1.5 1.2 cosine_convert_fusion
  2.7 0.3 copy.36
  3.0 0.1 convert_element_type.64
  3.1 4.2 %fusion.1 = (bf16[4,512,512]{2,1,0:T(8,128)(2,1)S(1)}, bf16[4,512,512]{2,1,0:T(8,128)(2,1)S(1)}) fusion(bf16[4,512,512]{2,1,0:T(8,128)(2,1)} %param.7, s32[4,512]{1,0:T(4,128)S(1)} %get-tuple-element.17, s32[4,512]{1,0:T(4,128)S(1)} %get-tuple-element.14, bf16[4,512,512]{2,1,0:T(8,128)(2,1)} %param.5, s32[4,512]{1,0:T(4,128)S(1)} %get-tuple-element.16, ...), kind=kLoop, calls=%fused_computation.8 | loop fusion | flops 8388608 | bytes 8421376 | tf_op jit(solution)/shard_map/jit(_where)/select_n | solution.py:29
  7.3 1.7 fusion.6
  9.0 1.8 reshape.176
  10.9 1.8 copy.37
  12.7 30.2 %all-to-all-start = ((bf16[128,2,4,512]{3,1,2,0:T(2,128)(2,1)}), bf16[128,2,4,512]{3,1,2,0:T(2,128)(2,1)S(1)}, u32[]{:S(2)}, u32[]{:S(2)}) async-start(bf16[128,2,4,512]{3,1,2,0:T(2,128)(2,1)} %copy.37), calls=%async_computation | async-start | bytes 2097152 | tf_op jit(solution)/shard_map/all_to_all | solution.py:68
  42.9 1.7 fusion.7
  44.6 1.8 reshape.179
  46.5 0.0 copy-start
  46.5 0.8 copy.40
  47.3 0.7 copy-done
  48.1 1.2 fusion.5
  49.3 1.7 fusion.8
  51.0 1.8 reshape.181
  52.9 0.8 copy.41
  53.7 3.2 %pad_maximum_fusion = bf16[128,4,4,512]{3,1,2,0:T(4,128)(2,1)} fusion(bf16[128,2,4,512]{3,1,2,0:T(2,128)(2,1)S(1)} %copy.41, bf16[128,2,4,512]{3,1,2,0:T(2,128)(2,1)S(1)} %copy.40), kind=kLoop, calls=%fused_computation.23 | loop fusion | flops 4194304 | bytes 4194304 | tf_op jit(solution)/shard_map/concatenate | solution.py:11
  56.9 39.6 %all-to-all-done = bf16[128,2,4,512]{3,1,2,0:T(2,128)(2,1)S(1)} async-done(((bf16[128,2,4,512]{3,1,2,0:T(2,128)(2,1)}), bf16[128,2,4,512]{3,1,2,0:T(2,128)(2,1)S(1)}, u32[]{:S(2)}, u32[]{:S(2)}) %all-to-all-start) | async-done | bytes 1048608 | tf_op jit(solution)/shard_map/all_to_all | solution.py:68
  96.5 9.1 %all-to-all-start.1 = ((bf16[128,4,4,512]{3,1,2,0:T(4,128)(2,1)}), bf16[128,4,4,512]{3,1,2,0:T(4,128)(2,1)S(1)}, u32[]{:S(2)}, u32[]{:S(2)}) async-start(bf16[128,4,4,512]{3,1,2,0:T(4,128)(2,1)} %pad_maximum_fusion), calls=%async_computation.1 | async-start | bytes 4194304 | tf_op jit(solution)/shard_map/all_to_all | solution.py:12
  105.7 2.5 fusion.30
  108.2 2.3 copy.51
  110.5 0.9 neg.23
  111.4 2.3 copy.50
  113.7 2.6 maximum_bitcast_fusion.12
  116.3 86.3 %all-to-all-done.1 = bf16[128,4,4,512]{3,1,2,0:T(4,128)(2,1)S(1)} async-done(((bf16[128,4,4,512]{3,1,2,0:T(4,128)(2,1)}), bf16[128,4,4,512]{3,1,2,0:T(4,128)(2,1)S(1)}, u32[]{:S(2)}, u32[]{:S(2)}) %all-to-all-start.1) | async-done | bytes 2097184 | tf_op jit(solution)/shard_map/all_to_all | solution.py:12
  202.6 1.5 fusion.29
  204.1 2.3 fusion.28
  206.4 0.1 copy.53
  206.5 0.1 copy_negate_fusion
  206.6 0.0 copy-start.1
  206.6 0.0 copy-start.2
  206.6 0.2 copy.63
  206.8 1.1 maximum_bitcast_fusion.14
  207.9 0.0 copy-done.1
  207.9 0.7 copy-done.2
  208.5 4.9 %fusion.18 = bf16[1,2,512,512]{2,3,1,0:T(8,128)(2,1)} fusion(bf16[1,1,2,512,512]{3,4,2,1,0:T(8,128)(2,1)S(1)} %copy-done.2, bf16[1,1,2,512,512]{3,4,2,1,0:T(8,128)(2,1)S(1)} %copy-done.1, bf16[1,1,2,512,512]{4,3,2,1,0:T(8,128)(2,1)} %maximum_bitcast_fusion.14, bf16[1,1,2,512,512]{4,3,2,1,0:T(8,128)(2,1)S(1)} %bitcast.104, ...), kind=kOutput, calls=%fused_computation.33 | convolution fusion | flops 2151677952 | bytes 6291456 | tf_op jit(solution)/shard_map/fcsu,fkcur->fksr/dot_general | solution.py:54
  213.4 2.5 copy.46
  215.9 64.1 %all_to_all.51 = bf16[1,2,512,512]{3,1,0,2:T(2,128)(2,1)S(1)} all-to-all(bf16[1,2,512,512]{3,1,0,2:T(2,128)(2,1)S(1)} %copy.46), channel_id=1, replica_groups=mesh['groups'=2,'freq'=128] {'freq'}, dimensions={2} | all-to-all | bytes 2097152 | tf_op jit(solution)/shard_map/all_to_all | solution.py:70
  280.1 0.4 copy.47
  280.5 0.3 copy.56
  280.8 2.1 multiply_convert_fusion
  (2 shorter events, 0.0 us)
Async XLA Ops:
  12.7 83.8 %all-to-all-start = ((bf16[128,2,4,512]{3,1,2,0:T(2,128)(2,1)}), bf16[128,2,4,512]{3,1,2,0:T(2,128)(2,1)S(1)}, u32[]{:S(2)}, u32[]{:S(2)}) async-start(bf16[128,2,4,512]{3,1,2,0:T(2,128)(2,1)} %copy.37), calls=%async_computation | async-start | bytes 2097152 | tf_op jit(solution)/shard_map/all_to_all | solution.py:68
  46.5 1.6 copy-start
  96.5 106.1 %all-to-all-start.1 = ((bf16[128,4,4,512]{3,1,2,0:T(4,128)(2,1)}), bf16[128,4,4,512]{3,1,2,0:T(4,128)(2,1)S(1)}, u32[]{:S(2)}, u32[]{:S(2)}) async-start(bf16[128,4,4,512]{3,1,2,0:T(4,128)(2,1)} %pad_maximum_fusion), calls=%async_computation.1 | async-start | bytes 4194304 | tf_op jit(solution)/shard_map/all_to_all | solution.py:12
  206.6 1.3 copy-start.1
  206.6 1.9 copy-start.2
where the time goes:
time: 284 us; the launch traced here: 283 us
  waiting for transfers between devices  126 us (44%)
  blocking collectives  64.1 us (23%)
  starting transfers between devices  39.4 us (14%)
  local copies, waits for them, and re-layouts  26.7 us (9%)
  other arithmetic  14.5 us (5%)
  matrix products  12.1 us (4%)
    all_to_all x1, waiting for transfers between devices, sent_together(): lax.all_to_all(both, axis, split_axis=split_dim, concat_axis=concat_dim,...  86.3 us
    all_to_all x1, blocking collectives, on_device(): lax.all_to_all(multiple, 'freq', split_axis=2, concat_axis=0, tiled=True)  64.1 us
    all_to_all x1, waiting for transfers between devices, on_device(): lax.all_to_all(spec_three, 'freq', split_axis=0, concat_axis=2, tiled=True)  39.6 us
    all_to_all x1, starting transfers between devices, on_device(): lax.all_to_all(spec_three, 'freq', split_axis=0, concat_axis=2, tiled=True)  30.2 us
    all_to_all x1, starting transfers between devices, sent_together(): lax.all_to_all(both, axis, split_axis=split_dim, concat_axis=concat_dim,...  9.15 us
    reshape x6, local copies, waits for them, and re-layouts, spectrum(): return spec.astype(jnp.bfloat16).reshape(count, 2, sources, receivers)  9.02 us
    unnamed x11, local copies, waits for them, and re-layouts  6.66 us
  transfers between devices with their start and end apart: 2, of which 2 were waited for; matrix products, arithmetic and copies ran while one was open for 8% of the time, Pallas kernels for 0%

commit v1 on v0

--- a/solution.py
+++ b/solution.py
@@ -4,6 +4,12 @@
 from jax.sharding import PartitionSpec as P
 
 F_DEV = 1
+
+
+def swap_blocks(value, axis, split, join):
+    shards = jnp.split(value, lax.axis_size(axis), axis=split)
+    received = lax.all_to_all(jnp.stack(shards), axis, 0, 0)
+    return jnp.concatenate(received, axis=join)
 
 
 def sent_together(arrays, axis, split_dim, concat_dim, along):
@@ -65,7 +71,7 @@
     spec_three = spectrum(primary_three, window_start[2], window_end[2], table, count)
     first, second = sent_together((spec_one, spec_two), "freq", 0, 2, 1)
     cross = correlate(first, second)
-    third = lax.all_to_all(spec_three, "freq", split_axis=0, concat_axis=2, tiled=True)
+    third = swap_blocks(spec_three, "freq", 0, 2)
     multiple = convolve(cross, third)
     piece = lax.all_to_all(multiple, "freq", split_axis=2, concat_axis=0, tiled=True)
     waves, parts, sources, receivers = piece.shape

time: 284 us -> 357 us (1.26)
  local copies, waits for them, and re-layouts: 26.7 us -> 101 us
    unnamed x11 -> x138, local copies, waits for them, and re-layouts: 6.66 us -> 82.9 us
    reshape x6 -> x4, local copies, waits for them, and re-layouts: 9.02 us -> 5.35 us  [spectrum(): return spec.astype(jnp.bfloat16).reshape(count, 2, sources, receivers)]
  transfers between devices with their start and end apart: 2 -> 2, of which waited for: 2 -> 2; matrix products, arithmetic and copies ran while one was open for 8% -> 7% of each run, Pallas kernels for 0% -> 0%
where the time goes in v1:
time: 357 us; the launch traced here: 356 us
  waiting for transfers between devices  126 us (35%)
  local copies, waits for them, and re-layouts  101 us (28%)
  blocking collectives  64.1 us (18%)
  starting transfers between devices  39.4 us (11%)
  other arithmetic  14.4 us (4%)
  matrix products  11.1 us (3%)
    all_to_all x1, waiting for transfers between devices, sent_together(): lax.all_to_all(both, axis, split_axis=split_dim, concat_axis=concat_dim,...  86.3 us
    unnamed x138, local copies, waits for them, and re-layouts  82.9 us
    all_to_all x1, blocking collectives, on_device(): lax.all_to_all(multiple, 'freq', split_axis=2, concat_axis=0, tiled=True)  64.1 us
    all_to_all x1, waiting for transfers between devices, swap_blocks(): received = lax.all_to_all(jnp.stack(shards), axis, 0, 0)  39.6 us
    all_to_all x1, starting transfers between devices, swap_blocks(): received = lax.all_to_all(jnp.stack(shards), axis, 0, 0)  30.2 us
    all_to_all x1, starting transfers between devices, sent_together(): lax.all_to_all(both, axis, split_axis=split_dim, concat_axis=concat_dim,...  9.15 us
  transfers between devices with their start and end apart: 2, of which 2 were waited for; matrix products, arithmetic and copies ran while one was open for 7% of the time, Pallas kernels for 0%

profile of v1, /device:TPU:35, one launch (start us, length us, event | category | flops | bytes accessed | tf_op | source)
XLA Modules:
  0.0 356.0 jit_solution(14491896108286407356)
XLA Ops:
  0.0 0.7 slice_bitcast_fusion.3
  0.7 0.7 slice_bitcast_fusion.2
  1.5 1.2 cosine_convert_fusion
  3.1 4.2 %fusion.1 = (bf16[4,512,512]{2,1,0:T(8,128)(2,1)S(1)}, bf16[4,512,512]{2,1,0:T(8,128)(2,1)S(1)}) fusion(bf16[4,512,512]{2,1,0:T(8,128)(2,1)} %param.7, s32[4,512]{1,0:T(4,128)S(1)} %get-tuple-element.145, s32[4,512]{1,0:T(4,128)S(1)} %get-tuple-element.142, bf16[4,512,512]{2,1,0:T(8,128)(2,1)} %param.5, s32[4,512]{1,0:T(4,128)S(1)} %get-tuple-element.144, ...), kind=kLoop, calls=%fused_computation.8 | loop fusion | flops 8388608 | bytes 8421376 | tf_op jit(solution)/shard_map/jit(_where)/select_n | solution.py:35
  7.3 0.7 fusion.6
  9.5 0.6 constant_dynamic-update-slice_fusion.126
  13.7 0.6 constant_dynamic-update-slice_fusion.119
  16.8 0.6 constant_dynamic-update-slice_fusion.114
  22.8 0.6 constant_dynamic-update-slice_fusion.104
  24.0 0.6 constant_dynamic-update-slice_fusion.102
  34.2 0.6 constant_dynamic-update-slice_fusion.85
  49.2 0.6 constant_dynamic-update-slice_fusion.60
  51.6 0.6 constant_dynamic-update-slice_fusion.56
  56.4 0.6 constant_dynamic-update-slice_fusion.48
  57.0 0.6 constant_dynamic-update-slice_fusion.47
  63.0 0.6 constant_dynamic-update-slice_fusion.37
  63.6 0.6 constant_dynamic-update-slice_fusion.36
  64.2 0.6 constant_dynamic-update-slice_fusion.35
  67.2 0.6 constant_dynamic-update-slice_fusion.30
  73.2 0.6 constant_dynamic-update-slice_fusion.20
  76.8 0.6 constant_dynamic-update-slice_fusion.14
  78.6 0.6 constant_dynamic-update-slice_fusion.11
  85.9 30.2 %all-to-all-start = ((bf16[128,1,2,4,512]{4,2,3,1,0:T(2,128)(2,1)}), bf16[128,1,2,4,512]{4,2,3,1,0:T(2,128)(2,1)S(1)}, u32[]{:S(2)}, u32[]{:S(2)}) async-start(bf16[128,1,2,4,512]{4,2,3,1,0:T(2,128)(2,1)} %constant_dynamic-update-slice_fusion), calls=%async_computation | async-start | bytes 2097152 | tf_op jit(solution)/shard_map/all_to_all | solution.py:11
  116.1 1.7 fusion.7
  117.8 1.8 reshape.440
  119.7 0.8 copy.548
  120.5 0.7 copy-done
  121.2 1.2 fusion.5
  122.5 1.7 fusion.8
  124.2 1.8 reshape.442
  126.0 0.8 copy.549
  126.9 3.2 pad_maximum_fusion
  130.1 39.6 %all-to-all-done = bf16[128,1,2,4,512]{4,2,3,1,0:T(2,128)(2,1)S(1)} async-done(((bf16[128,1,2,4,512]{4,2,3,1,0:T(2,128)(2,1)}), bf16[128,1,2,4,512]{4,2,3,1,0:T(2,128)(2,1)S(1)}, u32[]{:S(2)}, u32[]{:S(2)}) %all-to-all-start) | async-done | bytes 1048608 | tf_op jit(solution)/shard_map/all_to_all | solution.py:11
  169.7 9.1 %all-to-all-start.1 = ((bf16[128,4,4,512]{3,1,2,0:T(4,128)(2,1)}), bf16[128,4,4,512]{3,1,2,0:T(4,128)(2,1)S(1)}, u32[]{:S(2)}, u32[]{:S(2)}) async-start(bf16[128,4,4,512]{3,1,2,0:T(4,128)(2,1)} %pad_maximum_fusion), calls=%async_computation.1 | async-start | bytes 4194304 | tf_op jit(solution)/shard_map/all_to_all | solution.py:18
  178.8 2.5 fusion.30
  181.3 2.3 copy.559
  183.6 0.9 neg.23
  184.5 2.3 copy.558
  186.9 2.6 maximum_bitcast_fusion.12
  189.4 86.3 %all-to-all-done.1 = bf16[128,4,4,512]{3,1,2,0:T(4,128)(2,1)S(1)} async-done(((bf16[128,4,4,512]{3,1,2,0:T(4,128)(2,1)}), bf16[128,4,4,512]{3,1,2,0:T(4,128)(2,1)S(1)}, u32[]{:S(2)}, u32[]{:S(2)}) %all-to-all-start.1) | async-done | bytes 2097184 | tf_op jit(solution)/shard_map/all_to_all | solution.py:18
  275.8 1.5 fusion.29
  277.3 2.3 fusion.28
  279.9 1.1 maximum_bitcast_fusion.14
  281.0 0.7 copy-done.2
  281.7 4.9 %fusion.18 = bf16[1,2,512,512]{2,3,1,0:T(8,128)(2,1)} fusion(bf16[1,1,2,512,512]{3,4,2,1,0:T(8,128)(2,1)S(1)} %copy-done.2, bf16[1,1,2,512,512]{3,4,2,1,0:T(8,128)(2,1)S(1)} %copy-done.1, bf16[1,1,2,512,512]{4,3,2,1,0:T(8,128)(2,1)} %maximum_bitcast_fusion.14, bf16[1,1,2,512,512]{4,3,2,1,0:T(8,128)(2,1)S(1)} %bitcast.230, ...), kind=kOutput, calls=%fused_computation.33 | convolution fusion | flops 2151677952 | bytes 6291456 | tf_op jit(solution)/shard_map/fcsu,fkcur->fksr/dot_general | solution.py:60
  286.6 2.5 copy.554
  289.1 64.1 %all_to_all.38 = bf16[1,2,512,512]{3,1,0,2:T(2,128)(2,1)S(1)} all-to-all(bf16[1,2,512,512]{3,1,0,2:T(2,128)(2,1)S(1)} %copy.554), channel_id=1, replica_groups=mesh['groups'=2,'freq'=128] {'freq'}, dimensions={2} | all-to-all | bytes 2097152 | tf_op jit(solution)/shard_map/all_to_all | solution.py:76
  353.9 2.1 multiply_convert_fusion
  (131 shorter events, 68.8 us)
Async XLA Ops:
  85.9 83.8 %all-to-all-start = ((bf16[128,1,2,4,512]{4,2,3,1,0:T(2,128)(2,1)}), bf16[128,1,2,4,512]{4,2,3,1,0:T(2,128)(2,1)S(1)}, u32[]{:S(2)}, u32[]{:S(2)}) async-start(bf16[128,1,2,4,512]{4,2,3,1,0:T(2,128)(2,1)} %constant_dynamic-update-slice_fusion), calls=%async_computation | async-start | bytes 2097152 | tf_op jit(solution)/shard_map/all_to_all | solution.py:11
  119.6 1.6 copy-start
  169.7 106.1 %all-to-all-start.1 = ((bf16[128,4,4,512]{3,1,2,0:T(4,128)(2,1)}), bf16[128,4,4,512]{3,1,2,0:T(4,128)(2,1)S(1)}, u32[]{:S(2)}, u32[]{:S(2)}) async-start(bf16[128,4,4,512]{3,1,2,0:T(4,128)(2,1)} %pad_maximum_fusion), calls=%async_computation.1 | async-start | bytes 4194304 | tf_op jit(solution)/shard_map/all_to_all | solution.py:18
  279.8 1.3 copy-start.1
  279.8 1.9 copy-start.2
